TPU v7x, 32 devices: a whole 2x2x4 slice. The times are simulated.
32 devices in a mesh: rep: 4 (over y, core), tp: 8 (over z, x).
Axes of the slice: x: 2, y: 2, z: 4, core: 2. Of those that a mesh axis runs over, the one named last changes fastest.
Arguments:
- activations: bfloat16 [4, 2048, 4096], P('rep', 'tp'), may hold values from -6 to 6
- cotangent: bfloat16 [4, 2048, 8192], P('rep', None, 'tp'), may hold values from -0.13183594 to 0.13183594
- drift: bfloat16 [4, 4096, 8192], P('rep', None, 'tp'), may hold values from -8 to 8
- outer_weights: float32 [4096, 8192], P(('rep', 'tp')), may hold values from -6 to 6
- momentum: float32 [4096, 8192], P(('rep', 'tp')), may hold values from -6 to 6
Outputs:
- weights: bfloat16 [4096, 8192], P(None, 'tp')
- new_outer: float32 [4096, 8192], P(('rep', 'tp'))
- new_momentum: float32 [4096, 8192], P(('rep', 'tp'))
All inputs are finite; a program needn't handle non-finite values.
Results may differ from a plain program's by a relative error of at most 0.0085.
Values may be sent and summed in bfloat16 or wider, within the bound.
No kernel may reach another device: no remote copies, remote signals or barrier semaphores. Data moves between devices by JAX's collectives and lax.ppermute only.
A program may use at most 128 MiB of HBM per device.

v0:
```python
import jax
import jax.numpy as jnp
from jax import lax
from jax.sharding import PartitionSpec as P

outer_rate = 0.7
nesterov = 0.9


def on_device(activations, cotangent, drift, outer_weights, momentum):
    replicas = lax.axis_size("rep")
    cot_rows = cotangent[0]
    grad = jnp.einsum(
        "td,tf->df",
        lax.all_gather(activations, "tp", axis=1, tiled=True)[0],
        cot_rows,
        preferred_element_type=jnp.float32,
    )
    delta = lax.optimization_barrier((drift[0].astype(jnp.float32) + grad).astype(jnp.bfloat16))
    summed = lax.psum_scatter(
        delta.astype(jnp.float32).astype(jnp.bfloat16), "rep", scatter_dimension=0, tiled=True
    ).astype(jnp.float32)
    summed = lax.all_to_all(
        summed.astype(jnp.bfloat16), "tp", split_axis=0, concat_axis=1, tiled=True
    ).astype(summed.dtype)
    average = summed / replicas
    new_momentum = nesterov * momentum + average
    new_outer = outer_weights - outer_rate * (average + nesterov * new_momentum)
    rounded = new_outer.astype(jnp.bfloat16)
    spread = lax.all_to_all(rounded, "tp", split_axis=1, concat_axis=0, tiled=True)
    weights = lax.all_gather(spread, "rep", axis=0, tiled=True)
    return (weights, new_outer, new_momentum)


def solution(mesh):
    in_specs = (
        P("rep", "tp", None),
        P("rep", None, "tp"),
        P("rep", None, "tp"),
        P(("rep", "tp"), None),
        P(("rep", "tp"), None),
    )
    out_specs = (P(None, "tp"), P(("rep", "tp"), None), P(("rep", "tp"), None))
    return jax.shard_map(
        on_device, mesh=mesh, in_specs=in_specs, out_specs=out_specs, check_vma=False
    )
```

profile of v0, /device:TPU:0, one launch (start us, length us, event | category | flops | bytes accessed | tf_op | source)
XLA Modules:
  0.0 532.6 jit_solution(2489531201938662445)
XLA Ops:
  7.2 0.0 all-gather.3.cloned.1.call-start
  7.2 0.7 all-gather.3.cloned.1.call-update
  7.9 0.0 reduce-scatter.2.cloned.1.call-start
  7.9 232.2 %all-gather.3.cloned.1.call-done = bf16[1,2048,4096]{2,1,0:T(8,128)(2,1)} async-done(((bf16[1,256,4096]{2,1,0:T(8,128)(2,1)}), bf16[1,2048,4096]{2,1,0:T(8,128)(2,1)}) %all-gather.3.cloned.1.call-update) | async-done | bytes 16777232 | tf_op jit(solution)/shard_map/all_gather | solution.py:15
  240.1 25.8 %fusion = bf16[4096,1024]{1,0:T(8,128)(2,1)} fusion(bf16[1,4096,1024]{2,1,0:T(8,128)(2,1)} %param.7, bf16[1,2048,4096]{2,1,0:T(8,128)(2,1)} %all-gather.3.cloned.1.call-done, bf16[1,2048,1024]{2,1,0:T(8,128)(2,1)} %param.6), kind=kOutput, calls=%fused_computation.1 | convolution fusion | flops 17192452096 | bytes 37748736 | tf_op jit(solution)/shard_map/td,tf->df/dot_general | solution.py:13
  266.0 0.0 reduce-scatter.2.cloned.1.call-update
  266.0 69.8 %reduce-scatter.2.cloned.1.call-done = bf16[1024,1024]{1,0:T(8,128)(2,1)} async-done(((bf16[4096,1024]{1,0:T(8,128)(2,1)}), bf16[1024,1024]{1,0:T(8,128)(2,1)}) %reduce-scatter.2.cloned.1.call-update) | async-done | bytes 2097168 | tf_op jit(solution)/shard_map/reduce_scatter | solution.py:20
  335.7 5.5 %all-to-all-start = ((bf16[8,128,1024]{2,1,0:T(8,128)(2,1)}), bf16[8,128,1024]{2,1,0:T(8,128)(2,1)S(1)}, u32[]{:S(2)}, u32[]{:S(2)}) async-start(bf16[8,128,1024]{2,1,0:T(8,128)(2,1)} %bitcast.30), calls=%async_computation.1 | async-start | bytes 4194304 | tf_op jit(solution)/shard_map/all_to_all | solution.py:23
  341.2 0.2 all-gather.5.cloned.1.call-start
  341.5 5.6 %copy.13 = f32[128,8192]{0,1:T(8,128)} copy(f32[128,8192]{1,0:T(8,128)} %param.8) | data formatting | bytes 8388608 | tf_op args[3]
  347.0 5.6 %copy.12 = f32[128,8192]{0,1:T(8,128)} copy(f32[128,8192]{1,0:T(8,128)} %param.9) | data formatting | bytes 8388608 | tf_op args[4]
  352.6 36.7 %all-to-all-done = bf16[8,128,1024]{2,1,0:T(8,128)(2,1)S(1)} async-done(((bf16[8,128,1024]{2,1,0:T(8,128)(2,1)}), bf16[8,128,1024]{2,1,0:T(8,128)(2,1)S(1)}, u32[]{:S(2)}, u32[]{:S(2)}) %all-to-all-start) | async-done | bytes 2097184 | tf_op jit(solution)/shard_map/all_to_all | solution.py:23
  389.3 2.6 multiply_bitcast_fusion
  391.9 5.3 %copy.11 = f32[128,8,1024]{0,2,1:T(8,128)} copy(f32[128,8,1024]{2,0,1:T(8,128)} %multiply_bitcast_fusion) | data formatting | bytes 8388608 | tf_op jit(solution)/shard_map/div | solution.py:26
  397.3 9.7 %fusion.8 = (bf16[128,8192]{0,1:T(8,128)(2,1)}, f32[128,8192]{0,1:T(8,128)}, f32[128,8192]{0,1:T(8,128)}) fusion(f32[128,8192]{0,1:T(8,128)} %copy.13, f32[128,8192]{0,1:T(8,128)} %copy.12, f32[128,8,1024]{0,2,1:T(8,128)} %copy.11), kind=kLoop, calls=%fused_computation.10 | loop fusion | flops 7340032 | bytes 23068672 | tf_op jit(solution)/shard_map/convert_element_type | solution.py:29
  406.9 2.9 copy.14
  409.8 51.9 %all_to_all.32 = bf16[128,8,1024]{2,0,1:T(8,128)(2,1)} all-to-all(bf16[128,8,1024]{2,0,1:T(8,128)(2,1)S(1)} %copy.14), channel_id=1, replica_groups=mesh['rep'=4,'tp'=8] {'tp'}, dimensions={1} | all-to-all | bytes 4194304 | tf_op jit(solution)/shard_map/all_to_all | solution.py:30
  461.7 0.0 all-gather.5.cloned.1.call-update
  461.7 5.6 %copy.15 = f32[128,8192]{1,0:T(8,128)} copy(f32[128,8192]{0,1:T(8,128)} %get-tuple-element.7) | data formatting | bytes 8388608
  467.4 6.0 %copy.16 = f32[128,8192]{1,0:T(8,128)} copy(f32[128,8192]{0,1:T(8,128)} %get-tuple-element.8) | data formatting | bytes 8388608
  473.3 45.0 %all-gather.5.cloned.1.call-done = bf16[4096,1024]{1,0:T(8,128)(2,1)} async-done(((bf16[1024,1024]{1,0:T(8,128)(2,1)}), bf16[4096,1024]{1,0:T(8,128)(2,1)}) %all-gather.5.cloned.1.call-update) | async-done | bytes 8388624 | tf_op jit(solution)/shard_map/all_gather | solution.py:31
  518.3 7.8 %copy.18 = bf16[4096,1024]{1,0:T(8,128)(2,1)} copy(bf16[4096,1024]{1,0:T(8,128)(2,1)} %all-gather.5.cloned.1.call-done) | data formatting | bytes 16777216
Async XLA Ops:
  7.2 233.0 %all-gather.3.cloned.1.call-start = ((), (), s32[]{:S(2)}) async-start(), calls=%async_computation.3 | async-start | bytes 18874368 | tf_op jit(solution)/shard_map/all_gather | solution.py:15
  7.9 327.8 %reduce-scatter.2.cloned.1.call-start = ((), (), s32[]{:S(2)}) async-start(), calls=%async_computation.4 | async-start | bytes 10485760 | tf_op jit(solution)/shard_map/reduce_scatter | solution.py:20
  335.7 53.6 %all-to-all-start = ((bf16[8,128,1024]{2,1,0:T(8,128)(2,1)}), bf16[8,128,1024]{2,1,0:T(8,128)(2,1)S(1)}, u32[]{:S(2)}, u32[]{:S(2)}) async-start(bf16[8,128,1024]{2,1,0:T(8,128)(2,1)} %bitcast.30), calls=%async_computation.1 | async-start | bytes 4194304 | tf_op jit(solution)/shard_map/all_to_all | solution.py:23
  341.2 177.0 %all-gather.5.cloned.1.call-start = ((), (), s32[]{:S(2)}) async-start(), calls=%async_computation.5 | async-start | bytes 10485760 | tf_op jit(solution)/shard_map/all_gather | solution.py:31
Sparse Core Ops, SparseCore 0:
  10.1 229.9 all-gather.2
  266.1 69.5 reduce-scatter.1
  461.9 56.3 all-gather.4
where the time goes:
time: 533 us
  waiting for transfers between devices  384 us (72%)
  blocking collectives  51.9 us (10%)
  local copies, waits for them, and re-layouts  38.6 us (7%)
  matrix products  25.8 us (5%)
  between operations  13.8 us (3%)
  other arithmetic  12.3 us (2%)
  starting transfers between devices  5.8 us (1%)
    all_gather x1, waiting for transfers between devices, on_device(): lax.all_gather(activations, 'tp', axis=1, tiled=True)[0]  232 us
    reduce_scatter x1, waiting for transfers between devices, on_device(): lax.psum_scatter(delta.astype(jnp.float32).astype(jnp.bfloat16), 'rep', s...  69.8 us
    all_to_all x1, blocking collectives, on_device(): lax.all_to_all(rounded, 'tp', split_axis=1, concat_axis=0, tiled=True)  51.9 us
    all_gather x1, waiting for transfers between devices, on_device(): weights = lax.all_gather(spread, 'rep', axis=0, tiled=True)  45 us
    all_to_all x1, waiting for transfers between devices, on_device(): lax.all_to_all(summed.astype(jnp.bfloat16), 'tp', split_axis=0, concat_ax...  36.7 us
    unnamed x5, local copies, waits for them, and re-layouts  30.5 us
    dot_general x1, matrix products, on_device(): jnp.einsum('td,tf->df', lax.all_gather(activations, 'tp', axis=1, tiled=T...  25.8 us
  transfers between devices with their start and end apart: 4, of which 4 were waited for; matrix products, arithmetic and copies ran while one was open for 4% of the time, Pallas kernels for 0%

commit v1 on v0

--- a/solution.py
+++ b/solution.py
@@ -5,6 +5,13 @@
 
 outer_rate = 0.7
 nesterov = 0.9
+
+
+def trade_parts(x, mesh_axis, split, join):
+    count = lax.axis_size(mesh_axis)
+    pieces = jnp.stack(jnp.split(x, count, axis=split), axis=0)
+    pieces = lax.all_to_all(pieces, mesh_axis, split_axis=0, concat_axis=0)
+    return jnp.concatenate(pieces, axis=join)
 
 
 def on_device(activations, cotangent, drift, outer_weights, momentum):
@@ -20,9 +27,7 @@
     summed = lax.psum_scatter(
         delta.astype(jnp.float32).astype(jnp.bfloat16), "rep", scatter_dimension=0, tiled=True
     ).astype(jnp.float32)
-    summed = lax.all_to_all(
-        summed.astype(jnp.bfloat16), "tp", split_axis=0, concat_axis=1, tiled=True
-    ).astype(summed.dtype)
+    summed = trade_parts(summed.astype(jnp.bfloat16), "tp", 0, 1).astype(summed.dtype)
     average = summed / replicas
     new_momentum = nesterov * momentum + average
     new_outer = outer_weights - outer_rate * (average + nesterov * new_momentum)

time: 533 us -> 546 us (1.024)
  local copies, waits for them, and re-layouts: 38.6 us -> 51.8 us
    unnamed x5 -> x12, local copies, waits for them, and re-layouts: 30.5 us -> 42.1 us
where the time goes in v1:
time: 546 us; the launch traced here: 545 us
  waiting for transfers between devices  385 us (71%)
  local copies, waits for them, and re-layouts  51.8 us (9%)
  blocking collectives  51.8 us (9%)
  matrix products  25.8 us (5%)
  between operations  13.8 us (3%)
  other arithmetic  11.8 us (2%)
  starting transfers between devices  5.61 us (1%)
    all_gather x1, waiting for transfers between devices, on_device(): lax.all_gather(activations, 'tp', axis=1, tiled=True)[0]  232 us
    reduce_scatter x1, waiting for transfers between devices, on_device(): lax.psum_scatter(delta.astype(jnp.float32).astype(jnp.bfloat16), 'rep', s...  69.8 us
    all_to_all x1, blocking collectives, on_device(): lax.all_to_all(rounded, 'tp', split_axis=1, concat_axis=0, tiled=True)  51.8 us
    all_gather x1, waiting for transfers between devices, on_device(): weights = lax.all_gather(spread, 'rep', axis=0, tiled=True)  45 us
    unnamed x12, local copies, waits for them, and re-layouts  42.1 us
    all_to_all x1, waiting for transfers between devices, trade_parts(): pieces = lax.all_to_all(pieces, mesh_axis, split_axis=0, concat_axis=0)  36.9 us
    dot_general x1, matrix products, on_device(): jnp.einsum('td,tf->df', lax.all_gather(activations, 'tp', axis=1, tiled=T...  25.8 us
  transfers between devices with their start and end apart: 4, of which 4 were waited for; matrix products, arithmetic and copies ran while one was open for 4% of the time, Pallas kernels for 0%

profile of v1, /device:TPU:0, one launch (start us, length us, event | category | flops | bytes accessed | tf_op | source)
XLA Modules:
  0.0 545.1 jit_solution(16707470038937861957)
XLA Ops:
  7.2 0.0 all-gather.3.cloned.1.call-start
  7.2 0.7 all-gather.3.cloned.1.call-update
  7.9 0.0 reduce-scatter.2.cloned.1.call-start
  7.9 232.2 %all-gather.3.cloned.1.call-done = bf16[1,2048,4096]{2,1,0:T(8,128)(2,1)} async-done(((bf16[1,256,4096]{2,1,0:T(8,128)(2,1)}), bf16[1,2048,4096]{2,1,0:T(8,128)(2,1)}) %all-gather.3.cloned.1.call-update) | async-done | bytes 16777232 | tf_op jit(solution)/shard_map/all_gather | solution.py:22
  240.1 25.8 %fusion = bf16[4096,1024]{1,0:T(8,128)(2,1)} fusion(bf16[1,4096,1024]{2,1,0:T(8,128)(2,1)} %param.7, bf16[1,2048,4096]{2,1,0:T(8,128)(2,1)} %all-gather.3.cloned.1.call-done, bf16[1,2048,1024]{2,1,0:T(8,128)(2,1)} %param.6), kind=kOutput, calls=%fused_computation.1 | convolution fusion | flops 17192452096 | bytes 37748736 | tf_op jit(solution)/shard_map/td,tf->df/dot_general | solution.py:20
  266.0 0.0 reduce-scatter.2.cloned.1.call-update
  266.0 69.8 %reduce-scatter.2.cloned.1.call-done = bf16[1024,1024]{1,0:T(8,128)(2,1)} async-done(((bf16[4096,1024]{1,0:T(8,128)(2,1)}), bf16[1024,1024]{1,0:T(8,128)(2,1)}) %reduce-scatter.2.cloned.1.call-update) | async-done | bytes 2097168 | tf_op jit(solution)/shard_map/reduce_scatter | solution.py:27
  335.7 1.7 fusion.15
  337.4 1.7 fusion.14
  339.1 1.7 fusion.13
  340.8 1.7 fusion.12
  342.4 1.7 fusion.11
  344.1 1.7 fusion.10
  345.8 1.7 fusion.9
  347.4 1.7 fusion.8
  349.1 5.5 %all-to-all-start = ((bf16[8,128,1024]{2,1,0:T(8,128)(2,1)}), bf16[8,128,1024]{2,1,0:T(8,128)(2,1)S(1)}, u32[]{:S(2)}, u32[]{:S(2)}) async-start(bf16[8,128,1024]{2,1,0:T(8,128)(2,1)} %fusion.8), calls=%async_computation.1 | async-start | bytes 4194304 | tf_op jit(solution)/shard_map/all_to_all | solution.py:13
  354.6 0.0 all-gather.5.cloned.1.call-start
  354.6 5.6 %copy.11 = f32[128,8192]{0,1:T(8,128)} copy(f32[128,8192]{1,0:T(8,128)} %param.8) | data formatting | bytes 8388608 | tf_op args[3]
  360.2 5.6 %copy.10 = f32[128,8192]{0,1:T(8,128)} copy(f32[128,8192]{1,0:T(8,128)} %param.9) | data formatting | bytes 8388608 | tf_op args[4]
  365.8 36.9 %all-to-all-done = bf16[8,128,1024]{2,1,0:T(8,128)(2,1)S(1)} async-done(((bf16[8,128,1024]{2,1,0:T(8,128)(2,1)}), bf16[8,128,1024]{2,1,0:T(8,128)(2,1)S(1)}, u32[]{:S(2)}, u32[]{:S(2)}) %all-to-all-start) | async-done | bytes 2097184 | tf_op jit(solution)/shard_map/all_to_all | solution.py:13
  402.7 2.6 multiply_bitcast_fusion
  405.3 5.3 copy.9
  410.6 9.2 %fusion.16 = (bf16[128,8192]{0,1:T(8,128)(2,1)S(1)}, f32[128,8192]{0,1:T(8,128)}, f32[128,8192]{0,1:T(8,128)}) fusion(f32[128,8192]{0,1:T(8,128)} %copy.11, f32[128,8192]{0,1:T(8,128)} %copy.10, f32[128,8,1024]{0,2,1:T(8,128)} %copy.9), kind=kLoop, calls=%fused_computation.26 | loop fusion | flops 7340032 | bytes 23068672 | tf_op jit(solution)/shard_map/convert_element_type | solution.py:34
  419.8 51.8 %all_to_all.24 = bf16[128,8,1024]{0,2,1:T(8,128)(2,1)S(1)} all-to-all(bf16[128,8,1024]{0,2,1:T(8,128)(2,1)S(1)} %bitcast.60), channel_id=1, replica_groups=mesh['rep'=4,'tp'=8] {'tp'}, dimensions={1} | all-to-all | bytes 4194304 | tf_op jit(solution)/shard_map/all_to_all | solution.py:35
  471.6 2.6 copy.12
  474.3 0.0 all-gather.5.cloned.1.call-update
  474.3 5.6 %copy.13 = f32[128,8192]{1,0:T(8,128)} copy(f32[128,8192]{0,1:T(8,128)} %get-tuple-element.7) | data formatting | bytes 8388608
  479.9 6.0 %copy.14 = f32[128,8192]{1,0:T(8,128)} copy(f32[128,8192]{0,1:T(8,128)} %get-tuple-element.8) | data formatting | bytes 8388608
  485.9 45.0 %all-gather.5.cloned.1.call-done = bf16[4096,1024]{1,0:T(8,128)(2,1)} async-done(((bf16[1024,1024]{1,0:T(8,128)(2,1)}), bf16[4096,1024]{1,0:T(8,128)(2,1)}) %all-gather.5.cloned.1.call-update) | async-done | bytes 8388624 | tf_op jit(solution)/shard_map/all_gather | solution.py:36
  530.8 7.8 %copy.23 = bf16[4096,1024]{1,0:T(8,128)(2,1)} copy(bf16[4096,1024]{1,0:T(8,128)(2,1)} %all-gather.5.cloned.1.call-done) | data formatting | bytes 16777216
Async XLA Ops:
  7.2 233.0 %all-gather.3.cloned.1.call-start = ((), (), s32[]{:S(2)}) async-start(), calls=%async_computation.3 | async-start | bytes 18874368 | tf_op jit(solution)/shard_map/all_gather | solution.py:22
  7.9 327.8 %reduce-scatter.2.cloned.1.call-start = ((), (), s32[]{:S(2)}) async-start(), calls=%async_computation.4 | async-start | bytes 10485760 | tf_op jit(solution)/shard_map/reduce_scatter | solution.py:27
  349.1 53.6 %all-to-all-start = ((bf16[8,128,1024]{2,1,0:T(8,128)(2,1)}), bf16[8,128,1024]{2,1,0:T(8,128)(2,1)S(1)}, u32[]{:S(2)}, u32[]{:S(2)}) async-start(bf16[8,128,1024]{2,1,0:T(8,128)(2,1)} %fusion.8), calls=%async_computation.1 | async-start | bytes 4194304 | tf_op jit(solution)/shard_map/all_to_all | solution.py:13
  354.6 176.2 %all-gather.5.cloned.1.call-start = ((), (), s32[]{:S(2)}) async-start(), calls=%async_computation.5 | async-start | bytes 10485760 | tf_op jit(solution)/shard_map/all_gather | solution.py:36
Sparse Core Ops, SparseCore 0:
  10.1 229.9 all-gather.2
  266.1 69.5 reduce-scatter.1
  474.4 56.3 all-gather.4

commit v2 on v0

--- a/solution.py
+++ b/solution.py
@@ -5,6 +5,17 @@
 
 outer_rate = 0.7
 nesterov = 0.9
+
+
+def gather_by_hops(x, axis, dim):
+    peers = lax.axis_size(axis)
+    hops = [(i, (i + 1) % peers) for i in range(peers)]
+    pieces = [x]
+    for far in range(1, peers):
+        pieces = [lax.ppermute(pieces[0], axis, hops), *pieces]
+    whole = jnp.concatenate(pieces, axis=dim)
+    places = (lax.axis_index(axis) + 1) * pieces[-1].shape[dim]
+    return jnp.roll(whole, places, axis=dim)
 
 
 def on_device(activations, cotangent, drift, outer_weights, momentum):
@@ -28,7 +39,7 @@
     new_outer = outer_weights - outer_rate * (average + nesterov * new_momentum)
     rounded = new_outer.astype(jnp.bfloat16)
     spread = lax.all_to_all(rounded, "tp", split_axis=1, concat_axis=0, tiled=True)
-    weights = lax.all_gather(spread, "rep", axis=0, tiled=True)
+    weights = gather_by_hops(spread, "rep", 0)
     return (weights, new_outer, new_momentum)
 
 

time: 533 us -> 573 us (1.075)
  waiting for transfers between devices: 384 us -> 405 us
  local copies, waits for them, and re-layouts: 38.6 us -> 57.7 us
    ppermute x0 -> x3, waiting for transfers between devices: none -> 65.6 us  [gather_by_hops(): pieces = [lax.ppermute(pieces[0], axis, hops), *pieces]]
    all_gather x1 -> x0, waiting for transfers between devices: 45 us -> none  [on_device(): weights = lax.all_gather(spread, 'rep', axis=0, tiled=True)]
    unnamed x5 -> x15, local copies, waits for them, and re-layouts: 30.5 us -> 40.5 us
    dynamic_slice x0 -> x1, local copies, waits for them, and re-layouts: none -> 7.76 us  [gather_by_hops(): return jnp.roll(whole, places, axis=dim)]
  transfers between devices with their start and end apart: 4 -> 6, of which waited for: 4 -> 6; matrix products, arithmetic and copies ran while one was open for 4% -> 4% of each run, Pallas kernels for 0% -> 0%
where the time goes in v2:
time: 573 us; the launch traced here: 572 us
  waiting for transfers between devices  405 us (71%)
  local copies, waits for them, and re-layouts  57.7 us (10%)
  blocking collectives  52 us (9%)
  matrix products  25.8 us (5%)
  between operations  14.1 us (2%)
  other arithmetic  11.8 us (2%)
    all_gather x1, waiting for transfers between devices, on_device(): lax.all_gather(activations, 'tp', axis=1, tiled=True)[0]  232 us
    reduce_scatter x1, waiting for transfers between devices, on_device(): lax.psum_scatter(delta.astype(jnp.float32).astype(jnp.bfloat16), 'rep', s...  69.8 us
    ppermute x3, waiting for transfers between devices, gather_by_hops(): pieces = [lax.ppermute(pieces[0], axis, hops), *pieces]  65.6 us
    all_to_all x1, blocking collectives, on_device(): lax.all_to_all(rounded, 'tp', split_axis=1, concat_axis=0, tiled=True)  52 us
    unnamed x15, local copies, waits for them, and re-layouts  40.5 us
    all_to_all x1, waiting for transfers between devices, on_device(): lax.all_to_all(summed.astype(jnp.bfloat16), 'tp', split_axis=0, concat_ax...  36.9 us
    dot_general x1, matrix products, on_device(): jnp.einsum('td,tf->df', lax.all_gather(activations, 'tp', axis=1, tiled=T...  25.8 us
  transfers between devices with their start and end apart: 6, of which 6 were waited for; matrix products, arithmetic and copies ran while one was open for 4% of the time, Pallas kernels for 0%

profile of v2, /device:TPU:0, one launch (start us, length us, event | category | flops | bytes accessed | tf_op | source)
XLA Modules:
  0.0 572.2 jit_solution(15292368327214790420)
XLA Ops:
  7.2 0.0 all-gather.2.cloned.1.call-start
  7.2 0.7 all-gather.2.cloned.1.call-update
  7.9 0.0 reduce-scatter.2.cloned.1.call-start
  7.9 232.2 %all-gather.2.cloned.1.call-done = bf16[1,2048,4096]{2,1,0:T(8,128)(2,1)} async-done(((bf16[1,256,4096]{2,1,0:T(8,128)(2,1)}), bf16[1,2048,4096]{2,1,0:T(8,128)(2,1)}) %all-gather.2.cloned.1.call-update) | async-done | bytes 16777232 | tf_op jit(solution)/shard_map/all_gather | solution.py:26
  240.1 25.8 %fusion = bf16[4096,1024]{1,0:T(8,128)(2,1)} fusion(bf16[1,4096,1024]{2,1,0:T(8,128)(2,1)} %param.7, bf16[1,2048,4096]{2,1,0:T(8,128)(2,1)} %all-gather.2.cloned.1.call-done, bf16[1,2048,1024]{2,1,0:T(8,128)(2,1)} %param.6), kind=kOutput, calls=%fused_computation.1 | convolution fusion | flops 17192452096 | bytes 37748736 | tf_op jit(solution)/shard_map/td,tf->df/dot_general | solution.py:24
  266.0 0.0 reduce-scatter.2.cloned.1.call-update
  266.0 69.8 %reduce-scatter.2.cloned.1.call-done = bf16[1024,1024]{1,0:T(8,128)(2,1)} async-done(((bf16[4096,1024]{1,0:T(8,128)(2,1)}), bf16[1024,1024]{1,0:T(8,128)(2,1)}) %reduce-scatter.2.cloned.1.call-update) | async-done | bytes 2097168 | tf_op jit(solution)/shard_map/reduce_scatter | solution.py:31
  335.7 5.5 all-to-all-start
  341.2 5.6 copy.13
  346.8 5.6 copy.12
  352.4 36.9 %all-to-all-done = bf16[8,128,1024]{2,1,0:T(8,128)(2,1)S(1)} async-done(((bf16[8,128,1024]{2,1,0:T(8,128)(2,1)}), bf16[8,128,1024]{2,1,0:T(8,128)(2,1)S(1)}, u32[]{:S(2)}, u32[]{:S(2)}) %all-to-all-start) | async-done | bytes 2097184 | tf_op jit(solution)/shard_map/all_to_all | solution.py:34
  389.3 2.6 multiply_bitcast_fusion
  391.9 5.3 copy.11
  397.3 9.2 %fusion.8 = (bf16[128,8192]{0,1:T(8,128)(2,1)S(1)}, f32[128,8192]{0,1:T(8,128)}, f32[128,8192]{0,1:T(8,128)}) fusion(f32[128,8192]{0,1:T(8,128)} %copy.13, f32[128,8192]{0,1:T(8,128)} %copy.12, f32[128,8,1024]{0,2,1:T(8,128)} %copy.11), kind=kLoop, calls=%fused_computation.19 | loop fusion | flops 7340032 | bytes 23068672 | tf_op jit(solution)/shard_map/convert_element_type | solution.py:40
  406.5 2.6 copy.14
  409.1 52.0 %all_to_all.32 = bf16[128,8,1024]{2,0,1:T(8,128)(2,1)S(1)} all-to-all(bf16[128,8,1024]{2,0,1:T(8,128)(2,1)} %copy.14), channel_id=1, replica_groups=mesh['rep'=4,'tp'=8] {'tp'}, dimensions={1} | all-to-all | bytes 4194304 | tf_op jit(solution)/shard_map/all_to_all | solution.py:41
  461.1 0.0 collective-permute-start
  461.1 25.5 %collective-permute-done = bf16[1024,1024]{1,0:T(8,128)(2,1)S(1)} collective-permute-done((bf16[1024,1024]{1,0:T(8,128)(2,1)S(1)}, bf16[1024,1024]{1,0:T(8,128)(2,1)S(1)}, u32[]{:S(2)}, u32[]{:S(2)}) %collective-permute-start) | collective-permute-done | bytes 2097184 | tf_op jit(solution)/shard_map/ppermute | solution.py:15
  486.5 0.0 copy-start
  486.5 1.3 copy-done
  487.9 0.0 collective-permute-start.1
  487.9 25.6 %collective-permute-done.1 = bf16[1024,1024]{1,0:T(8,128)(2,1)} collective-permute-done((bf16[1024,1024]{1,0:T(8,128)(2,1)S(1)}, bf16[1024,1024]{1,0:T(8,128)(2,1)}, u32[]{:S(2)}, u32[]{:S(2)}) %collective-permute-start.1) | collective-permute-done | bytes 2097184 | tf_op jit(solution)/shard_map/ppermute | solution.py:15
  513.4 0.0 collective-permute-start.2
  513.4 5.6 copy.15
  519.0 5.6 copy.16
  524.6 0.0 copy-start.1
  524.6 14.6 %collective-permute-done.2 = bf16[1024,1024]{1,0:T(8,128)(2,1)} collective-permute-done((bf16[1024,1024]{1,0:T(8,128)(2,1)}, bf16[1024,1024]{1,0:T(8,128)(2,1)}, u32[]{:S(2)}, u32[]{:S(2)}) %collective-permute-start.2) | collective-permute-done | bytes 2097184 | tf_op jit(solution)/shard_map/ppermute | solution.py:15
  539.2 3.1 constant_dynamic-update-slice_fusion.7
  542.3 3.1 constant_dynamic-update-slice_fusion.6
  545.4 0.0 copy-done.1
  545.4 1.5 constant_dynamic-update-slice_fusion.5
  546.9 1.5 constant_dynamic-update-slice_fusion.4
  548.4 3.1 constant_dynamic-update-slice_fusion.3
  551.5 3.1 constant_dynamic-update-slice_fusion.2
  554.6 1.5 constant_dynamic-update-slice_fusion.1
  556.1 1.5 constant_dynamic-update-slice_fusion
  557.6 7.8 %constant_dynamic-slice_fusion = bf16[4096,1024]{1,0:T(8,128)(2,1)} fusion(bf16[8192,1024]{1,0:T(8,128)(2,1)} %constant_dynamic-update-slice_fusion, s32[]{:T(128)S(6)} %select_n.14), kind=kLoop, calls=%fused_computation.18 | loop fusion | bytes 16777220 | tf_op jit(solution)/shard_map/jit(_roll_dynamic)/dynamic_slice | solution.py:18
Async XLA Ops:
  7.2 233.0 %all-gather.2.cloned.1.call-start = ((), (), s32[]{:S(2)}) async-start(), calls=%async_computation.3 | async-start | bytes 18874368 | tf_op jit(solution)/shard_map/all_gather | solution.py:26
  7.9 327.8 %reduce-scatter.2.cloned.1.call-start = ((), (), s32[]{:S(2)}) async-start(), calls=%async_computation.4 | async-start | bytes 10485760 | tf_op jit(solution)/shard_map/reduce_scatter | solution.py:31
  335.7 53.6 %all-to-all-start = ((bf16[8,128,1024]{2,1,0:T(8,128)(2,1)}), bf16[8,128,1024]{2,1,0:T(8,128)(2,1)S(1)}, u32[]{:S(2)}, u32[]{:S(2)}) async-start(bf16[8,128,1024]{2,1,0:T(8,128)(2,1)} %bitcast.32), calls=%async_computation.1 | async-start | bytes 4194304 | tf_op jit(solution)/shard_map/all_to_all | solution.py:34
  461.1 25.5 %collective-permute-start = (bf16[1024,1024]{1,0:T(8,128)(2,1)S(1)}, bf16[1024,1024]{1,0:T(8,128)(2,1)S(1)}, u32[]{:S(2)}, u32[]{:S(2)}) collective-permute-start(bf16[1024,1024]{1,0:T(8,128)(2,1)S(1)} %bitcast.28), channel_id=1, source_target_pairs={{0,8},{8,16},{16,24},{24,0},{1,9},{9,17},{17,25},{25,1},{2,10},{10... | collective-permute-start | bytes 6291464 | tf_op jit(solution)/shard_map/ppermute | solution.py:15
  486.5 1.3 copy-start
  487.9 25.6 %collective-permute-start.1 = (bf16[1024,1024]{1,0:T(8,128)(2,1)S(1)}, bf16[1024,1024]{1,0:T(8,128)(2,1)}, u32[]{:S(2)}, u32[]{:S(2)}) collective-permute-start(bf16[1024,1024]{1,0:T(8,128)(2,1)S(1)} %collective-permute-done), channel_id=1, source_target_pairs={{0,8},{8,16},{16,24},{24,0},{1,9},{9,17},{17,25},{25,1},{2,10},{10... | collective-permute-start | bytes 6291464 | tf_op jit(solution)/shard_map/ppermute | solution.py:15
  513.4 25.8 %collective-permute-start.2 = (bf16[1024,1024]{1,0:T(8,128)(2,1)}, bf16[1024,1024]{1,0:T(8,128)(2,1)}, u32[]{:S(2)}, u32[]{:S(2)}) collective-permute-start(bf16[1024,1024]{1,0:T(8,128)(2,1)} %collective-permute-done.1), channel_id=1, source_target_pairs={{0,8},{8,16},{16,24},{24,0},{1,9},{9,17},{17,25},{25,1},{2,10},{10... | collective-permute-start | bytes 6291464 | tf_op jit(solution)/shard_map/ppermute | solution.py:15
  524.6 20.8 %copy-start.1 = (bf16[1024,1024]{1,0:T(8,128)(2,1)S(1)}, bf16[1024,1024]{1,0:T(8,128)(2,1)}, u32[]{:S(2)}) copy-start(bf16[1024,1024]{1,0:T(8,128)(2,1)} %copy-done) | copy-start | bytes 6291460
Sparse Core Ops, SparseCore 0:
  10.1 229.9 all-gather.1
  266.1 69.5 reduce-scatter.1
